TPU v7x, 128 devices: a whole 4x4x4 slice. The times are simulated.
128 devices in a mesh: dp: 8 (over x, y_lo), vocab: 16 (over z, y_hi, core).
Axes of the slice: x: 4, y: 4 (y_hi: 2, y_lo: 2; y = y_hi * 2 + y_lo), z: 4, core: 2. Of those that a mesh axis runs over, the one named last changes fastest.
Arguments:
- hidden: bfloat16 [8192, 5120], P(('dp', 'vocab')), may hold values from -100 to 100
- tokens: int32 [8192], P('dp'), may hold values from 0 to 18431
- old_weight: bfloat16 [18432, 5120], P('vocab'), may hold values from -1 to 1
- new_weight: bfloat16 [18432, 5120], P('dp', 'vocab'), may hold values from -6 to 6
Outputs:
- logprob: float32 [8192], P(('dp', 'vocab'))
- engine_weight: bfloat16 [18432, 5120], P('vocab')
All inputs are finite; a program needn't handle non-finite values.
Results may differ from a plain program's by a relative error of at most 0.001.
Values may be sent and summed in bfloat16 or wider, within the bound.
A program may use at most 128 MiB of HBM per device.

v0:
```python
import jax
import jax.numpy as jnp
from jax import lax
from jax.sharding import Mesh
from jax.sharding import PartitionSpec as P

DP = ("dp_0", "dp_1")
DP_VOCAB = ("dp_0", "dp_1", "vocab")


def sent_together(arrays, axis, split_dim, concat_dim, along):
    ends, at = ([], 0)
    for a in arrays[:-1]:
        at += a.shape[along]
        ends.append(at)
    both = jnp.concatenate(arrays, axis=along)
    return tuple(
        jnp.split(
            lax.all_to_all(both, axis, split_axis=split_dim, concat_axis=concat_dim, tiled=True),
            ends,
            axis=along,
        )
    )


def whole_of(shard, axes, dim):
    if not axes:
        return shard
    nearer = lax.all_gather(shard, axes[-1], axis=dim, tiled=True)
    return whole_of(nearer, axes[:-1], dim)


def on_device(hidden, tokens, old_weight, new_weight):
    ranks = lax.axis_size("vocab")
    rank = lax.axis_index("vocab")
    vocab_rows = old_weight.shape[0]
    first_id = rank * vocab_rows
    own_rows = hidden.shape[0]
    logits = lax.dot_general(
        lax.all_gather(hidden, "vocab", axis=0, tiled=True),
        old_weight,
        (((1,), (1,)), ((), ())),
        preferred_element_type=jnp.float32,
    )
    highest = jnp.max(logits, axis=1)
    summed = jnp.sum(jnp.exp(logits - highest[:, None]), axis=1)
    wanted = tokens - first_id
    columns = lax.broadcasted_iota(jnp.int32, logits.shape, 1)
    target = jnp.sum(jnp.where(columns == wanted[:, None], logits, 0.0), axis=1)
    stats = jnp.stack([highest, summed, target], axis=0)
    highest, summed, target = (stats[0], stats[1], stats[2])
    shaped = (
        highest.reshape(ranks, own_rows),
        summed.reshape(ranks, own_rows),
        target.reshape(ranks, own_rows),
    )
    got_high, got_sum, got_target = sent_together(
        (shaped[0], shaped[1], shaped[2]), "vocab", 0, 0, 1
    )
    highest = jnp.max(got_high, axis=0)
    summed = jnp.sum(got_sum * jnp.exp(got_high - highest[None, :]), axis=0)
    target = jnp.sum(got_target, axis=0)
    logprob = target - highest - jnp.log(summed)
    replicas = lax.axis_size(DP)
    trainer_cols = new_weight.shape[1]
    owned = lax.all_to_all(
        lax.all_to_all(new_weight, DP, split_axis=1, concat_axis=0, tiled=True),
        "vocab",
        split_axis=0,
        concat_axis=1,
        tiled=True,
    )
    owner_count = owned.shape[0]
    shaped_pieces = owned.reshape(owner_count, ranks, 1, trainer_cols // replicas)
    complete = whole_of(shaped_pieces, DP, 2)
    engine_weight = complete.reshape(owner_count, ranks * trainer_cols)
    return (logprob, engine_weight)


def solution(mesh):
    finer = Mesh(mesh.devices.reshape(4, 2, mesh.shape["vocab"]), ("dp_0", "dp_1", "vocab"))
    return jax.shard_map(
        on_device,
        mesh=finer,
        in_specs=(P(DP_VOCAB, None), P(DP), P("vocab", None), P(DP, "vocab")),
        out_specs=(P(DP_VOCAB), P("vocab", None)),
        check_vma=False,
    )
```

profile of v0, /device:TPU:1, one launch (start us, length us, event | category | flops | bytes accessed | tf_op | source)
XLA Modules:
  0.0 325.5 jit_solution(2934551947676968886)
XLA Ops:
  7.2 0.0 all-gather.9.cloned.1.call-start
  7.2 24.7 %all_to_all.44 = bf16[2304,8,40]{0,2,1:T(8,128)(2,1)S(1)} all-to-all(bf16[2304,8,40]{0,2,1:T(8,128)(2,1)} %bitcast.16), channel_id=1, replica_groups=mesh['dp_0'=4,'dp_1'=2,'vocab'=16] {'dp_0','dp_1'}, dimensions={1} | all-to-all | bytes 2949120 | tf_op jit(solution)/shard_map/all_to_all | solution.py:67
  31.9 0.2 copy.9
  32.2 0.5 all_to_all.38
  32.7 0.3 copy.10
  33.0 31.0 %all_to_all.45 = bf16[16,1152,40]{1,2,0:T(8,128)(2,1)S(1)} all-to-all(bf16[16,1152,40]{1,2,0:T(8,128)(2,1)S(1)} %copy.10), channel_id=1, replica_groups=mesh['dp_0'=4,'dp_1'=2,'vocab'=16] {'vocab'}, dimensions={0} | all-to-all | bytes 2949120 | tf_op jit(solution)/shard_map/all_to_all | solution.py:66
  64.0 1.3 copy.11
  65.3 0.0 all-gather.5.cloned.1.call-start
  65.3 0.7 all-gather.5.cloned.1.call-update
  66.0 0.0 all-gather.7.cloned.1.call-start
  66.1 40.3 %all-gather.9.cloned.1.call-done = bf16[1152,16,80]{0,1,2:T(8,128)(2,1)} async-done(((bf16[1152,16,40]{0,1,2:T(8,128)(2,1)}), bf16[1152,16,80]{0,1,2:T(8,128)(2,1)}) %all-gather.9.cloned.1.call-update) | async-done | bytes 2949136 | tf_op jit(solution)/shard_map/all_gather | solution.py:29
  106.3 4.0 %copy.12 = bf16[1152,16,80]{0,2,1:T(8,128)(2,1)} copy(bf16[1152,16,80]{0,1,2:T(8,128)(2,1)} %all-gather.9.cloned.1.call-done) | data formatting | bytes 5898240 | tf_op jit(solution)/shard_map/all_gather | solution.py:29
  110.4 81.7 %all-gather.5.cloned.1.call-done = bf16[1024,5120]{1,0:T(8,128)(2,1)} async-done(((bf16[64,5120]{1,0:T(8,128)(2,1)}), bf16[1024,5120]{1,0:T(8,128)(2,1)}) %all-gather.5.cloned.1.call-update) | async-done | bytes 10485776 | tf_op jit(solution)/shard_map/all_gather | solution.py:40
  192.1 19.5 %fusion.1 = (f32[1024]{0:T(1024)S(1)}, f32[1024,1152]{1,0:T(8,128)}) fusion(bf16[1024,5120]{1,0:T(8,128)(2,1)} %all-gather.5.cloned.1.call-done, bf16[1152,5120]{1,0:T(8,128)(2,1)} %param.6), kind=kOutput, calls=%fused_computation.11 | convolution fusion | flops 12080774144 | bytes 27004928 | tf_op jit(solution)/shard_map/dot_general | solution.py:39
  211.5 0.1 reshape_squeeze_stack.9
  211.6 3.1 exponential_reduce_fusion
  214.8 0.1 reshape_squeeze_stack.10
  214.8 0.1 reshape_squeeze_stack.11
  214.9 0.1 pad_maximum_fusion
  215.0 10.4 %all_to_all.46 = f32[16,1,192]{2,1,0:T(1,128)S(1)} all-to-all(f32[16,1,192]{2,1,0:T(1,128)S(1)} %all_to_all.32), channel_id=1, replica_groups=mesh['dp_0'=4,'dp_1'=2,'vocab'=16] {'vocab'}, dimensions={0} | all-to-all | bytes 24576 | tf_op jit(solution)/shard_map/all_to_all | solution.py:19
  225.4 0.1 slice_reduce_fusion
  225.5 0.5 log_subtract_fusion
  226.0 76.7 %all-gather.7.cloned.1.call-done = bf16[1152,16,8,40]{0,3,2,1:T(8,128)(2,1)} async-done(((bf16[1152,16,2,40]{0,3,2,1:T(8,128)(2,1)}), bf16[1152,16,8,40]{0,3,2,1:T(8,128)(2,1)}) %all-gather.7.cloned.1.call-update) | async-done | bytes 11796496 | tf_op jit(solution)/shard_map/all_gather | solution.py:29
  302.7 16.3 %copy.13 = bf16[1152,5120]{1,0:T(8,128)(2,1)} copy(bf16[1152,5120]{0,1:T(8,128)(2,1)} %bitcast.12) | data formatting | bytes 23592960
  (8 shorter events, 0.1 us)
Async XLA Ops:
  7.2 99.1 %all-gather.9.cloned.1.call-start = ((), (), s32[]{:S(2)}) async-start(), calls=%async_computation.5 | async-start | bytes 4423680 | tf_op jit(solution)/shard_map/all_gather | solution.py:29
  65.2 45.1 %copy-start = (s32[1024]{0:T(1024)S(1)}, s32[1024]{0:T(1024)}, u32[]{:S(2)}) copy-start(s32[1024]{0:T(1024)} %param.5) | copy-start | bytes 12292
  65.3 126.8 %all-gather.5.cloned.1.call-start = ((), (), s32[]{:S(2)}) async-start(), calls=%async_computation.3 | async-start | bytes 11141120 | tf_op jit(solution)/shard_map/all_gather | solution.py:40
  66.0 236.7 %all-gather.7.cloned.1.call-start = ((), (), s32[]{:S(2)}) async-start(), calls=%async_computation.4 | async-start | bytes 14745600 | tf_op jit(solution)/shard_map/all_gather | solution.py:29
Sparse Core Ops, SparseCore 0:
  65.4 40.8 all-gather.8
  108.8 83.2 all-gather.4
  193.7 108.8 all-gather.6
where the time goes:
time: 326 us; the launch traced here: 325 us
  waiting for transfers between devices  199 us (61%)
  blocking collectives  66 us (20%)
  local copies, waits for them, and re-layouts  22.8 us (7%)
  matrix products  19.5 us (6%)
  between operations  13.8 us (4%)
  other arithmetic  3.87 us (1%)
    all_gather x2, waiting for transfers between devices, whole_of(): nearer = lax.all_gather(shard, axes[-1], axis=dim, tiled=True)  117 us
    all_gather x1, waiting for transfers between devices, on_device(): lax.all_gather(hidden, 'vocab', axis=0, tiled=True)  81.7 us
    all_to_all x1, blocking collectives, on_device(): lax.all_to_all(lax.all_to_all(new_weight, DP, split_axis=1, concat_axis=0...  31 us
    all_to_all x1, blocking collectives, on_device(): lax.all_to_all(new_weight, DP, split_axis=1, concat_axis=0, tiled=True)  24.7 us
    dot_general x1, matrix products, on_device(): lax.dot_general(lax.all_gather(hidden, 'vocab', axis=0, tiled=True), old_...  19.5 us
    unnamed x4, local copies, waits for them, and re-layouts  16.3 us
    all_to_all x1, blocking collectives, sent_together(): lax.all_to_all(both, axis, split_axis=split_dim, concat_axis=concat_dim,...  10.4 us
  transfers between devices with their start and end apart: 3, of which 3 were waited for; matrix products, arithmetic and copies ran while one was open for 8% of the time, Pallas kernels for 0%

commit v1 on v0

--- a/solution.py
+++ b/solution.py
@@ -36,8 +36,14 @@
     vocab_rows = old_weight.shape[0]
     first_id = rank * vocab_rows
     own_rows = hidden.shape[0]
+
+    def _recover_flows(row_data):
+        y1 = jnp.stack([row_data for _ in range(lax.axis_size("vocab"))], axis=0)
+        tall = lax.all_to_all(y1, "vocab", 0, 0)
+        return jnp.concatenate(tall, axis=0)
+
     logits = lax.dot_general(
-        lax.all_gather(hidden, "vocab", axis=0, tiled=True),
+        _recover_flows(hidden),
         old_weight,
         (((1,), (1,)), ((), ())),
         preferred_element_type=jnp.float32,

time: 326 us -> 300 us (0.920)
  waiting for transfers between devices: 199 us -> 159 us
  starting transfers between devices: 0.12 us -> 7.64 us
  local copies, waits for them, and re-layouts: 22.8 us -> 28.2 us
    all_to_all x0 -> x1, waiting for transfers between devices: none -> 118 us  [_recover_flows(): tall = lax.all_to_all(y1, 'vocab', 0, 0)]
    all_gather x1 -> x0, waiting for transfers between devices: 81.7 us -> none  [on_device(): lax.all_gather(hidden, 'vocab', axis=0, tiled=True)]
    all_gather x2, waiting for transfers between devices: 117 us -> 41 us  [whole_of(): nearer = lax.all_gather(shard, axes[-1], axis=dim, tiled=True)]
    all_to_all x0 -> x1, starting transfers between devices: none -> 7.57 us  [_recover_flows(): tall = lax.all_to_all(y1, 'vocab', 0, 0)]
    another operation x0 -> x1, local copies, waits for them, and re-layouts: none -> 5.4 us  [_recover_flows(): y1 = jnp.stack([row_data for _ in range(lax.axis_size('vocab'))], axis=0)]
    unnamed x4 -> x6, local copies, waits for them, and re-layouts: 16.3 us -> 16.3 us
  transfers between devices with their start and end apart: 3 -> 3, of which waited for: 3 -> 2; matrix products, arithmetic and copies ran while one was open for 8% -> 10% of each run, Pallas kernels for 0% -> 0%
where the time goes in v1:
time: 300 us; the launch traced here: 299 us
  waiting for transfers between devices  159 us (53%)
  blocking collectives  66.9 us (22%)
  local copies, waits for them, and re-layouts  28.2 us (9%)
  matrix products  19.5 us (6%)
  between operations  14.1 us (5%)
  starting transfers between devices  7.64 us (3%)
  other arithmetic  3.87 us (1%)
    all_to_all x1, waiting for transfers between devices, _recover_flows(): tall = lax.all_to_all(y1, 'vocab', 0, 0)  118 us
    all_gather x2, waiting for transfers between devices, whole_of(): nearer = lax.all_gather(shard, axes[-1], axis=dim, tiled=True)  41 us
    all_to_all x1, blocking collectives, on_device(): lax.all_to_all(lax.all_to_all(new_weight, DP, split_axis=1, concat_axis=0...  31 us
    all_to_all x1, blocking collectives, on_device(): lax.all_to_all(new_weight, DP, split_axis=1, concat_axis=0, tiled=True)  24.7 us
    dot_general x1, matrix products, on_device(): lax.dot_general(_recover_flows(hidden), old_weight, (((1,), (1,)), ((), (...  19.5 us
    unnamed x6, local copies, waits for them, and re-layouts  16.3 us
    all_to_all x1, blocking collectives, sent_together(): lax.all_to_all(both, axis, split_axis=split_dim, concat_axis=concat_dim,...  11.2 us
    all_to_all x1, starting transfers between devices, _recover_flows(): tall = lax.all_to_all(y1, 'vocab', 0, 0)  7.57 us
  transfers between devices with their start and end apart: 3, of which 2 were waited for; matrix products, arithmetic and copies ran while one was open for 10% of the time, Pallas kernels for 0%

profile of v1, /device:TPU:1, one launch (start us, length us, event | category | flops | bytes accessed | tf_op | source)
XLA Modules:
  0.0 299.5 jit_solution(362709147990168644)
XLA Ops:
  7.2 0.0 all-gather.6.cloned.1.call-start
  7.2 24.7 %all_to_all.49 = bf16[2304,8,40]{0,2,1:T(8,128)(2,1)S(1)} all-to-all(bf16[2304,8,40]{0,2,1:T(8,128)(2,1)} %bitcast.17), channel_id=1, replica_groups=mesh['dp_0'=4,'dp_1'=2,'vocab'=16] {'dp_0','dp_1'}, dimensions={1} | all-to-all | bytes 2949120 | tf_op jit(solution)/shard_map/all_to_all | solution.py:73
  31.9 0.2 copy.9
  32.2 0.5 all_to_all.42
  32.7 0.3 copy.10
  33.0 31.0 %all_to_all.50 = bf16[16,1152,40]{1,2,0:T(8,128)(2,1)S(1)} all-to-all(bf16[16,1152,40]{1,2,0:T(8,128)(2,1)S(1)} %copy.10), channel_id=1, replica_groups=mesh['dp_0'=4,'dp_1'=2,'vocab'=16] {'vocab'}, dimensions={0} | all-to-all | bytes 2949120 | tf_op jit(solution)/shard_map/all_to_all | solution.py:72
  64.0 1.3 copy.11
  65.2 0.0 all-gather.6.cloned.1.call-update
  65.3 0.0 all-gather.4.cloned.1.call-start
  65.3 41.0 %all-gather.6.cloned.1.call-done = bf16[1152,16,80]{0,1,2:T(8,128)(2,1)} async-done(((bf16[1152,16,40]{0,1,2:T(8,128)(2,1)}), bf16[1152,16,80]{0,1,2:T(8,128)(2,1)}) %all-gather.6.cloned.1.call-update) | async-done | bytes 2949136 | tf_op jit(solution)/shard_map/all_gather | solution.py:29
  106.3 4.0 %copy.12 = bf16[1152,16,80]{0,2,1:T(8,128)(2,1)} copy(bf16[1152,16,80]{0,1,2:T(8,128)(2,1)} %all-gather.6.cloned.1.call-done) | data formatting | bytes 5898240 | tf_op jit(solution)/shard_map/all_gather | solution.py:29
  110.3 5.4 %stack.2 = bf16[16,64,5120]{2,1,0:T(8,128)(2,1)} broadcast(bf16[64,5120]{1,0:T(8,128)(2,1)S(1)} %copy-done), dimensions={1,2} | broadcast | bytes 11141120 | tf_op jit(solution)/shard_map/stack | solution.py:41
  115.7 7.6 %all-to-all-start = ((bf16[16,64,5120]{2,1,0:T(8,128)(2,1)}), bf16[16,64,5120]{2,1,0:T(8,128)(2,1)}, u32[]{:S(2)}, u32[]{:S(2)}) async-start(bf16[16,64,5120]{2,1,0:T(8,128)(2,1)} %stack.2), calls=%async_computation | async-start | bytes 20971520 | tf_op jit(solution)/shard_map/all_to_all | solution.py:42
  123.3 118.3 %all-to-all-done = bf16[16,64,5120]{2,1,0:T(8,128)(2,1)} async-done(((bf16[16,64,5120]{2,1,0:T(8,128)(2,1)}), bf16[16,64,5120]{2,1,0:T(8,128)(2,1)}, u32[]{:S(2)}, u32[]{:S(2)}) %all-to-all-start) | async-done | bytes 10485792 | tf_op jit(solution)/shard_map/all_to_all | solution.py:42
  241.6 19.5 %fusion.1 = (f32[1024]{0:T(1024)S(1)}, f32[1024,1152]{1,0:T(8,128)}) fusion(bf16[1024,5120]{1,0:T(8,128)(2,1)} %bitcast, bf16[1152,5120]{1,0:T(8,128)(2,1)} %param.6), kind=kOutput, calls=%fused_computation.11 | convolution fusion | flops 12080774144 | bytes 27004928 | tf_op jit(solution)/shard_map/dot_general | solution.py:45
  261.1 0.1 reshape_squeeze_stack.9
  261.2 3.1 %exponential_reduce_fusion = (f32[1024]{0:T(1024)S(1)}, f32[1024]{0:T(1024)S(1)}) fusion(f32[1024,1152]{1,0:T(8,128)} %get-tuple-element.11, f32[1024]{0:T(1024)S(1)} %get-tuple-element.10, s32[1024]{0:T(1024)S(1)} %broadcast_subtract_fusion), kind=kLoop, calls=%fused_computation.2 | loop fusion | flops 5896192 | bytes 4734976 | tf_op jit(solution)/shard_map/reduce_sum | solution.py:52
  264.3 0.1 reshape_squeeze_stack.10
  264.4 0.1 reshape_squeeze_stack.11
  264.5 0.1 pad_maximum_fusion
  264.6 11.2 %all_to_all.51 = f32[16,1,192]{2,1,0:T(1,128)S(1)} all-to-all(f32[16,1,192]{2,1,0:T(1,128)S(1)} %all_to_all.36), channel_id=1, replica_groups=mesh['dp_0'=4,'dp_1'=2,'vocab'=16] {'vocab'}, dimensions={0} | all-to-all | bytes 24576 | tf_op jit(solution)/shard_map/all_to_all | solution.py:19
  275.8 0.1 slice_reduce_fusion
  275.8 0.5 log_subtract_fusion
  276.4 16.3 %copy.13 = bf16[1152,5120]{1,0:T(8,128)(2,1)} copy(bf16[1152,5120]{0,1:T(8,128)(2,1)} %bitcast.13) | data formatting | bytes 23592960
  (10 shorter events, 0.1 us)
Async XLA Ops:
  7.2 99.1 %all-gather.6.cloned.1.call-start = ((), (), s32[]{:S(2)}) async-start(), calls=%async_computation.5 | async-start | bytes 4423680 | tf_op jit(solution)/shard_map/all_gather | solution.py:29
  65.2 45.1 %copy-start = (bf16[64,5120]{1,0:T(8,128)(2,1)S(1)}, bf16[64,5120]{1,0:T(8,128)(2,1)}, u32[]{:S(2)}) copy-start(bf16[64,5120]{1,0:T(8,128)(2,1)} %param.4) | copy-start | bytes 1966084
  65.3 211.1 %all-gather.4.cloned.1.call-start = ((), (), s32[]{:S(2)}) async-start(), calls=%async_computation.4 | async-start | bytes 14745600 | tf_op jit(solution)/shard_map/all_gather | solution.py:29
  115.7 7.6 %copy-start.1 = (s32[1024]{0:T(1024)S(1)}, s32[1024]{0:T(1024)}, u32[]{:S(2)}) copy-start(s32[1024]{0:T(1024)} %param.5) | copy-start | bytes 12292
  115.7 125.9 %all-to-all-start = ((bf16[16,64,5120]{2,1,0:T(8,128)(2,1)}), bf16[16,64,5120]{2,1,0:T(8,128)(2,1)}, u32[]{:S(2)}, u32[]{:S(2)}) async-start(bf16[16,64,5120]{2,1,0:T(8,128)(2,1)} %stack.2), calls=%async_computation | async-start | bytes 20971520 | tf_op jit(solution)/shard_map/all_to_all | solution.py:42
Sparse Core Ops, SparseCore 0:
  65.4 40.8 all-gather.5
  110.4 112.8 all-gather.3
